TPU v7x, 32 devices: a whole 2x2x4 slice. The times are simulated.
32 devices in a mesh: grp: 4 (over y, x), chan: 8 (over z, core).
Axes of the slice: x: 2, y: 2, z: 4, core: 2. Of those that a mesh axis runs over, the one named last changes fastest.
Arguments:
- visibilities: float32 [4, 2, 8, 16, 2, 2048], P('grp', None, 'chan'), may hold values from -12 to 12
- model: bfloat16 [4, 2, 8, 8, 16, 2, 2048], P('grp', None, None, 'chan'), may hold values from -6 to 6
- flags: int32 [4, 8, 16, 2, 2048], P('grp', 'chan'), may hold values 0 or 1
- antennas: int32 [4, 2, 2048], P('grp'), may hold values from 0 to 63, as said below
- correlation: int32 [4, 4, 40], replicated, may hold values from -1 to 63, as said below
- gains_init: float32 [4, 2, 8, 8, 16, 64], P('grp', None, None, 'chan'), may hold values from -4 to 4
Outputs:
- final_jones_matrices: float32 [4, 2, 8, 8, 16, 64], P('grp', None, None, 'chan')
- consensus: float32 [4, 2, 8, 8, 16, 64], P('grp', None, None, 'chan')
- residual_vis: float32 [4, 2, 8, 16, 2, 2048], P('grp', None, 'chan')
Inputs may be any that keep to these rules, and one draw needn't show every extreme that they name: antennas[g, 0, b] and antennas[g, 1, b] are different slots. correlation[g, h, j] and correlation[h, g, j] are the slots in clusters g and h of one shared station, or both -1; the live entries of a list are a prefix of it and distinct; correlation[g, g] is all -1; each pair of clusters shares 40 // 2 to 40 stations, and some pair exactly 40.
All inputs are finite; a program needn't handle non-finite values. No bound on the sum of `flags` on one device may be relied on, other than what follows from the above.
Results may differ from a plain program's by a relative error of at most 0.0003.
Values sent between devices are 32-bit elements; how exact they have to be, the bound alone decides.
A program may use at most 64 MiB of HBM per device.

v0:
```python
import jax
import jax.numpy as jnp
from jax import lax
from jax.sharding import PartitionSpec as P

ITERS = 2


def poly_basis(count):
    freq = jnp.arange(count, dtype=jnp.float32)
    xval = (2.0 * freq + 1.0) / count - 1.0
    return jnp.stack([jnp.ones_like(xval), xval, 1.5 * xval * xval - 0.5], axis=1)


def gram_inverse(basis):
    gram = jnp.dot(basis.T, basis, precision=lax.Precision.HIGHEST)
    cross_one = jnp.cross(gram[1], gram[2])
    cross_two = jnp.cross(gram[2], gram[0])
    cross_three = jnp.cross(gram[0], gram[1])
    determinant = jnp.sum(gram[0] * cross_one)
    return jnp.stack([cross_one, cross_two, cross_three], axis=1) / determinant


def model_terms(leading_receiver_jones, trailing_receiver_jones, vis, model, flag):
    model_re = model[0].astype(jnp.float32)
    model_im = model[1].astype(jnp.float32)
    weight = (1 - flag).astype(jnp.float32)
    prod_re = (
        leading_receiver_jones[0] * trailing_receiver_jones[0]
        + leading_receiver_jones[1] * trailing_receiver_jones[1]
    )
    prod_im = (
        leading_receiver_jones[1] * trailing_receiver_jones[0]
        - leading_receiver_jones[0] * trailing_receiver_jones[1]
    )
    pred_re = prod_re * model_re - prod_im * model_im
    pred_im = prod_re * model_im + prod_im * model_re
    res_re = weight * (vis[0] - jnp.sum(pred_re, axis=0))
    res_im = weight * (vis[1] - jnp.sum(pred_im, axis=0))
    return (model_re, model_im, weight, pred_re, pred_im, res_re, res_im)


def station_sides(leading_receiver_jones, trailing_receiver_jones, terms):
    model_re, model_im, weight, pred_re, pred_im, res_re, res_im = terms
    resid_re = res_re + weight * pred_re
    resid_im = res_im + weight * pred_im
    zed_re = trailing_receiver_jones[0] * model_re + trailing_receiver_jones[1] * model_im
    zed_im = trailing_receiver_jones[0] * model_im - trailing_receiver_jones[1] * model_re
    ups_re = leading_receiver_jones[0] * model_re - leading_receiver_jones[1] * model_im
    ups_im = leading_receiver_jones[0] * model_im + leading_receiver_jones[1] * model_re
    first_station_side = jnp.stack(
        [
            jnp.sum(resid_re * zed_re + resid_im * zed_im, axis=-2),
            jnp.sum(resid_im * zed_re - resid_re * zed_im, axis=-2),
            jnp.sum(weight * (zed_re * zed_re + zed_im * zed_im), axis=-2),
        ]
    )
    second_station_side = jnp.stack(
        [
            jnp.sum(resid_re * ups_re + resid_im * ups_im, axis=-2),
            jnp.sum(resid_re * ups_im - resid_im * ups_re, axis=-2),
            jnp.sum(weight * (ups_re * ups_re + ups_im * ups_im), axis=-2),
        ]
    )
    return (first_station_side, second_station_side)


def new_gains(summed_totals, target, penalty):
    return jnp.stack(
        [
            (summed_totals[0] + penalty * target[0]) / (summed_totals[2] + penalty),
            (summed_totals[1] + penalty * target[1]) / (summed_totals[2] + penalty),
        ]
    )


def on_device(visibilities, model, flags, antennas, correlation, gains_init):
    high = lax.Precision.HIGHEST
    vis = visibilities[0]
    coherence = model[0]
    flagged = flags[0]
    stations_of = antennas[0]
    start_gains = gains_init[0]
    per_device = start_gains.shape[2]
    slots = start_gains.shape[-1]
    penalty = 2.0 * vis.shape[-1] * vis.shape[-2] / slots
    all_channels = per_device * lax.axis_size("chan")
    basis_all = poly_basis(all_channels)
    ginv = gram_inverse(basis_all)
    projector = jnp.dot(jnp.dot(basis_all, ginv, precision=high), basis_all.T, precision=high)
    iota = jnp.arange(slots, dtype=jnp.int32)
    leading_receiver_picker = (stations_of[0][:, None] == iota[None, :]).astype(jnp.float32)
    trailing_receiver_picker = (stations_of[1][:, None] == iota[None, :]).astype(jnp.float32)
    cluster_index = lax.axis_index("grp")
    mine = lax.dynamic_slice_in_dim(correlation, cluster_index, 1, 0)[0]
    select = (mine[:, :, None] == iota[None, None, :]).astype(jnp.float32)
    count = jnp.sum(select, axis=(0, 1))

    def spread_over_interferometer_pairs(receiver_choice_matrix, final_jones_matrices):
        flat = final_jones_matrices.reshape(-1, slots)
        picked = lax.dot_general(
            flat, receiver_choice_matrix, (((1,), (1,)), ((), ())), precision=high
        )
        return picked.reshape(
            final_jones_matrices.shape[:-1] + (1, receiver_choice_matrix.shape[0])
        )

    def to_stations(side, receiver_choice_matrix):
        flat = side.reshape(-1, side.shape[-1])
        return jnp.dot(flat, receiver_choice_matrix, precision=high).reshape(
            side.shape[:-1] + (slots,)
        )

    def consensus_values(values):
        moved = jnp.moveaxis(values, 2, 0)
        rows = moved.reshape(per_device, -1)
        whole = lax.all_to_all(rows, "chan", split_axis=1, concat_axis=0, tiled=True)
        smooth = jnp.dot(projector, whole, precision=high)
        back = lax.all_to_all(smooth, "chan", split_axis=0, concat_axis=1, tiled=True)
        return jnp.moveaxis(back.reshape(moved.shape), 0, 2)

    present_jones_matrices = start_gains
    dual = jnp.zeros_like(start_gains)
    agreed = consensus_values(present_jones_matrices)
    for step in range(ITERS):
        local_leading_receiver_jones = spread_over_interferometer_pairs(
            leading_receiver_picker, present_jones_matrices
        )
        local_trailing_receiver_jones = spread_over_interferometer_pairs(
            trailing_receiver_picker, present_jones_matrices
        )
        local_terms = model_terms(
            local_leading_receiver_jones, local_trailing_receiver_jones, vis, coherence, flagged
        )
        first_station_side, second_station_side = station_sides(
            local_leading_receiver_jones, local_trailing_receiver_jones, local_terms
        )
        summed_totals = to_stations(first_station_side, leading_receiver_picker) + to_stations(
            second_station_side, trailing_receiver_picker
        )
        updated = new_gains(summed_totals, agreed - dual, penalty)
        early = consensus_values(updated + dual)
        gain_rows = updated.reshape(-1, slots)
        average_rows = jnp.concatenate([gain_rows, early.reshape(-1, slots)], axis=0)
        outgoing = jnp.einsum("hjs,rs->hjr", select, average_rows, precision=high)
        received = lax.all_to_all(outgoing, "grp", split_axis=0, concat_axis=0, tiled=True)
        added = jnp.einsum("hjs,hjr->rs", select, received, precision=high)
        joined = (average_rows + added) / (1.0 + count)
        present_jones_matrices = joined[: gain_rows.shape[0]].reshape(updated.shape)
        agreed = joined[gain_rows.shape[0] :].reshape(early.shape)
        dual = dual + present_jones_matrices - agreed
    leading_receiver_jones = spread_over_interferometer_pairs(
        leading_receiver_picker, present_jones_matrices
    )
    trailing_receiver_jones = spread_over_interferometer_pairs(
        trailing_receiver_picker, present_jones_matrices
    )
    terms = model_terms(leading_receiver_jones, trailing_receiver_jones, vis, coherence, flagged)
    residual_vis = jnp.stack([terms[5], terms[6]])
    return (present_jones_matrices[None], agreed[None], residual_vis[None])


def solution(mesh):
    return jax.shard_map(
        on_device,
        mesh=mesh,
        in_specs=(
            P("grp", None, "chan", None, None, None),
            P("grp", None, None, "chan", None, None, None),
            P("grp", "chan", None, None, None),
            P("grp", None, None),
            P(),
            P("grp", None, None, "chan", None, None),
        ),
        out_specs=(
            P("grp", None, None, "chan", None, None),
            P("grp", None, None, "chan", None, None),
            P("grp", None, "chan", None, None, None),
        ),
        check_vma=False,
    )
```

profile of v0, /device:TPU:0, one launch (start us, length us, event | category | flops | bytes accessed | tf_op | source)
XLA Modules:
  0.0 154.5 jit_solution(10395948544894003127)
XLA Ops:
  0.7 1.7 %all_to_all.70 = f32[1,8,2048]{2,0,1:T(1,128)} reshape(f32[1,2,8,1,16,64]{5,4,3,2,1,0:T(8,128)} %param.13) | data formatting | bytes 131072 | tf_op jit(solution)/shard_map/all_to_all | solution.py:117
  2.4 6.4 %all-to-all-start = ((f32[1,8,2048]{2,0,1:T(1,128)}), f32[1,8,2048]{2,0,1:T(1,128)S(1)}, u32[]{:S(2)}, u32[]{:S(2)}) async-start(f32[1,8,2048]{2,0,1:T(1,128)} %all_to_all.70), calls=%async_computation | async-start | bytes 131072 | tf_op jit(solution)/shard_map/all_to_all | solution.py:117
  9.6 1.9 %convolution_bitcast_fusion = f32[256,2048]{1,0:T(8,128)S(1)} fusion(f32[256,64]{1,0:T(8,128)} %bitcast.329, s32[2048]{0:T(1024)S(1)} %bitcast.352), kind=kOutput, calls=%fused_computation.52 | convolution fusion | flops 402784256 | bytes 2170880 | tf_op jit(solution)/shard_map/dot_general | solution.py:101
  38.1 1.5 fusion.129
  39.9 1.3 fusion.39
  41.7 6.7 %add_reduce_fusion.2 = (f32[8,16,2048]{2,1,0:T(8,128)}, f32[8,16,2048]{2,1,0:T(8,128)}, f32[8,16,2048]{2,1,0:T(8,128)S(1)}, f32[8,16,2048]{2,1,0:T(8,128)S(1)}, ...) fusion(f32[8,16,2048]{2,1,0:T(8,128)S(1)} %bitcast.322, f32[8,16,2048]{2,1,0:T(8,128)S(1)} %bitcast.321, ...), kind=kLoop, calls=%fused_computation.83 | loop fusion | flops 24641536 | bytes 15466496 | tf_op jit(solution)/shard_map/reduce_sum | solution.py:60
  48.4 2.3 %fusion = f32[3,8,16,64]{3,2,1,0:T(8,128)} fusion(f32[1,8,1,16,2048]{4,3,1,0,2:T(8,128)S(1)} %bitcast.344, f32[1,8,1,16,2048]{4,3,1,0,2:T(8,128)S(1)} %bitcast.342, f32[1,8,1,16,2048]{4,3,1,0,2:T(8,128)S(1)} %bitcast.343, s32[2048]{0:T(1024)S(1)} %bitcast.348), kind=kOutput, calls=%fused_computation.29 | convolution fusion | flops 605683712 | bytes 3252224 | tf_op jit(solution)/shard_map/dot_general | solution.py:110
  53.5 5.1 %all-to-all-start.1 = ((f32[8,1,2048]{2,1,0:T(1,128)}), f32[8,1,2048]{2,1,0:T(1,128)S(1)}, u32[]{:S(2)}, u32[]{:S(2)}) async-start(f32[8,1,2048]{2,1,0:T(1,128)} %copy.78), calls=%async_computation.1 | async-start | bytes 131072 | tf_op jit(solution)/shard_map/all_to_all | solution.py:119
  58.6 3.9 %fusion.41 = f32[3,8,16,64]{3,2,1,0:T(8,128)} fusion(f32[3,8,16,64]{3,2,1,0:T(8,128)} %fusion, f32[1,8,1,16,2048]{4,3,1,0,2:T(8,128)} %bitcast.335, f32[1,8,1,16,2048]{4,3,1,0,2:T(8,128)} %bitcast.334, f32[1,8,1,16,2048]{4,3,1,0,2:T(8,128)S(1)} %bitcast.333, s32[2048]{0:T(1024)S(1)} %bitcast.353), kind=kOutput, calls=%fused_computation.94 | convolution fusion | flops 605708288 | bytes 3350528 | tf_op jit(solution)/shard_map/dot_general | solution.py:110
  62.4 2.1 %all-to-all-done.1 = f32[8,1,2048]{2,1,0:T(1,128)S(1)} async-done(((f32[8,1,2048]{2,1,0:T(1,128)}), f32[8,1,2048]{2,1,0:T(1,128)S(1)}, u32[]{:S(2)}, u32[]{:S(2)}) %all-to-all-start.1) | async-done | bytes 65568 | tf_op jit(solution)/shard_map/all_to_all | solution.py:119
  66.0 8.7 %all_to_all.95 = f32[1,8,2048]{2,0,1:T(1,128)S(1)} all-to-all(f32[1,8,2048]{2,0,1:T(1,128)S(1)} %all_to_all.86), channel_id=1, replica_groups=mesh['grp'=4,'chan'=8] {'chan'}, dimensions={1} | all-to-all | bytes 131072 | tf_op jit(solution)/shard_map/all_to_all | solution.py:117
  75.6 3.4 %all-to-all-start.3 = ((f32[8,1,2048]{2,1,0:T(1,128)}), f32[8,1,2048]{2,1,0:T(1,128)S(1)}, u32[]{:S(2)}, u32[]{:S(2)}) async-start(f32[8,1,2048]{2,1,0:T(1,128)} %copy.80), calls=%async_computation.3 | async-start | bytes 131072 | tf_op jit(solution)/shard_map/all_to_all | solution.py:119
  79.1 5.7 %all-to-all-done.3 = f32[8,1,2048]{2,1,0:T(1,128)S(1)} async-done(((f32[8,1,2048]{2,1,0:T(1,128)}), f32[8,1,2048]{2,1,0:T(1,128)S(1)}, u32[]{:S(2)}, u32[]{:S(2)}) %all-to-all-start.3) | async-done | bytes 65568 | tf_op jit(solution)/shard_map/all_to_all | solution.py:119
  85.2 1.1 fusion.79
  86.2 3.7 %all-to-all-start.4 = ((f32[4,40,512]{2,1,0:T(8,128)}), f32[4,40,512]{2,1,0:T(8,128)S(1)}, u32[]{:S(2)}, u32[]{:S(2)}) async-start(f32[4,40,512]{2,1,0:T(8,128)} %fusion.79), calls=%async_computation.4 | async-start | bytes 655360 | tf_op jit(solution)/shard_map/all_to_all | solution.py:146
  90.1 5.6 %all-to-all-done.4 = f32[4,40,512]{2,1,0:T(8,128)S(1)} async-done(((f32[4,40,512]{2,1,0:T(8,128)}), f32[4,40,512]{2,1,0:T(8,128)S(1)}, u32[]{:S(2)}, u32[]{:S(2)}) %all-to-all-start.4) | async-done | bytes 327712 | tf_op jit(solution)/shard_map/all_to_all | solution.py:146
  97.1 1.0 fusion.52
  98.1 1.5 fusion.127
  99.6 1.4 multiply_add_fusion.5
  101.0 1.5 fusion.126
  104.1 1.6 %copy.84 = f32[256,64]{1,0:T(8,128)} copy(f32[256,64]{0,1:T(8,128)} %get-tuple-element.77) | data formatting | bytes 131072 | tf_op jit(solution)/shard_map/slice | solution.py:149
  105.7 2.8 %fusion.37 = (f32[16,2,2048]{2,0,1:T(8,128)S(1)}, f32[16,2,2048]{2,0,1:T(8,128)S(1)}) fusion(f32[8,16,2048]{2,1,0:T(8,128)} %get-tuple-element.48, f32[8,16,2048]{2,1,0:T(8,128)S(1)} %get-tuple-element.47, bf16[1,1,8,1,16,2,2048]{6,5,4,3,2,1,0:T(2,128)(2,1)S(1)} %get-tuple-element.58, bf16[1,1,8,1,16,2,2048]{6,5,4,3,2,1,0:T(2,128)(2,1)S(1)} %get-tuple-element.57), kind=kLoop, calls=%fused_computation.90 | loop fusion | flops 5111808 | bytes 4718592 | tf_op jit(solution)/shard_map/reduce_sum | solution.py:38
  110.1 4.9 %add_reduce_fusion = (f32[8,16,2048]{2,1,0:T(8,128)S(1)}, f32[8,16,2048]{2,1,0:T(8,128)S(1)}, f32[8,16,2048]{2,1,0:T(8,128)S(1)}, f32[8,16,2048]{2,1,0:T(8,128)S...) fusion(f32[8,16,2048]{2,1,0:T(8,128)S(1)} %bitcast.326, f32[8,16,2048]{2,1,0:T(8,128)S(1)} %bitcast.325, ...), kind=kLoop, calls=%fused_computation.75 | loop fusion | flops 24641536 | bytes 15466496 | tf_op jit(solution)/shard_map/reduce_sum | solution.py:60
  115.0 1.6 %fusion.10 = f32[3,8,16,64]{3,2,1,0:T(8,128)S(1)} fusion(f32[1,8,1,16,2048]{4,3,1,0,2:T(8,128)S(1)} %bitcast.341, f32[1,8,1,16,2048]{4,3,1,0,2:T(8,128)S(1)} %bitcast.339, f32[1,8,1,16,2048]{4,3,1,0,2:T(8,128)S(1)} %bitcast.340, s32[2048]{0:T(1024)S(1)} %bitcast.350), kind=kOutput, calls=%fused_computation.41 | convolution fusion | flops 605683712 | bytes 3252224 | tf_op jit(solution)/shard_map/dot_general | solution.py:110
  116.6 1.6 %fusion.40 = f32[3,8,16,64]{3,2,1,0:T(8,128)S(1)} fusion(f32[3,8,16,64]{3,2,1,0:T(8,128)S(1)} %fusion.10, f32[1,8,1,16,2048]{4,3,1,0,2:T(8,128)S(1)} %bitcast.338, f32[1,8,1,16,2048]{4,3,1,0,2:T(8,128)S(1)} %bitcast.337, f32[1,8,1,16,2048]{4,3,1,0,2:T(8,128)S(1)} %bitcast.336, s32[2048]{0:T(1024)S(1)} %bitcast.355), kind=kOutput, calls=%fused_computation.93 | convolution fusion | flops 605708288 | bytes 3350528 | tf_op jit(solution)/shard_map/dot_general | solution.py:110
  118.7 8.3 %all_to_all.96 = f32[1,8,2048]{2,0,1:T(1,128)S(1)} all-to-all(f32[1,8,2048]{2,0,1:T(1,128)S(1)} %copy.86), channel_id=1, replica_groups=mesh['grp'=4,'chan'=8] {'chan'}, dimensions={1} | all-to-all | bytes 131072 | tf_op jit(solution)/shard_map/all_to_all | solution.py:117
  127.9 3.6 %all-to-all-start.6 = ((f32[8,1,2048]{2,1,0:T(1,128)}), f32[8,1,2048]{2,1,0:T(1,128)S(1)}, u32[]{:S(2)}, u32[]{:S(2)}) async-start(f32[8,1,2048]{2,1,0:T(1,128)} %copy.87), calls=%async_computation.6 | async-start | bytes 131072 | tf_op jit(solution)/shard_map/all_to_all | solution.py:119
  131.6 5.5 %all-to-all-done.6 = f32[8,1,2048]{2,1,0:T(1,128)S(1)} async-done(((f32[8,1,2048]{2,1,0:T(1,128)}), f32[8,1,2048]{2,1,0:T(1,128)S(1)}, u32[]{:S(2)}, u32[]{:S(2)}) %all-to-all-start.6) | async-done | bytes 65568 | tf_op jit(solution)/shard_map/all_to_all | solution.py:119
  137.8 9.1 %all_to_all.97 = f32[4,40,512]{2,1,0:T(8,128)S(1)} all-to-all(f32[4,40,512]{2,1,0:T(8,128)S(1)} %fusion.77), channel_id=1, replica_groups=mesh['grp'=4,'chan'=8] {'grp'}, dimensions={0} | all-to-all | bytes 655360 | tf_op jit(solution)/shard_map/all_to_all | solution.py:146
  147.2 1.0 fusion.46
  149.8 1.5 fusion.33
  151.8 1.2 copy.94
  (124 shorter events, 21.7 us)
Async XLA Ops:
  0.6 78.4 %copy-start = (s32[4,4,40]{2,1,0:T(4,128)S(1)}, s32[4,4,40]{2,1,0:T(4,128)}, u32[]{:S(2)}) copy-start(s32[4,4,40]{2,1,0:T(4,128)} %param.12) | copy-start | bytes 7684
  0.6 10.8 %copy-start.16 = (f32[1,2,8,1,16,64]{5,4,3,2,1,0:T(8,128)S(1)}, f32[1,2,8,1,16,64]{5,4,3,2,1,0:T(8,128)}, u32[]{:S(2)}) copy-start(f32[1,2,8,1,16,64]{5,4,3,2,1,0:T(8,128)} %param.13) | copy-start | bytes 196612
  2.4 50.2 %all-to-all-start = ((f32[1,8,2048]{2,0,1:T(1,128)}), f32[1,8,2048]{2,0,1:T(1,128)S(1)}, u32[]{:S(2)}, u32[]{:S(2)}) async-start(f32[1,8,2048]{2,0,1:T(1,128)} %all_to_all.70), calls=%async_computation | async-start | bytes 131072 | tf_op jit(solution)/shard_map/all_to_all | solution.py:117
  9.5 86.5 %copy-start.21 = (s32[1,1,2048]{2,1,0:T(1,128)}, s32[1,1,2048]{2,1,0:T(1,128)S(1)}, u32[]{:S(2)}) copy-start(s32[1,1,2048]{2,1,0:T(1,128)S(1)} %get-tuple-element.78) | copy-start | bytes 24580
  13.2 24.9 %copy-start.15 = (bf16[1,2,8,1,16,2,2048]{6,5,4,3,2,1,0:T(2,128)(2,1)S(1)}, bf16[1,2,8,1,16,2,2048]{6,5,4,3,2,1,0:T(2,128)(2,1)}, u32[]{:S(2)}) copy-start(bf16[1,2,8,1,16,2,2048]{6,5,4,3,2,1,0:T(2,128)(2,1)} %param.9) | copy-start | bytes 6291460
  38.0 1.5 copy-start.19
  38.0 1.6 %copy-start.2 = (s32[1,1,16,2,2048]{4,3,2,1,0:T(2,128)S(1)}, s32[1,1,16,2,2048]{4,3,2,1,0:T(2,128)}, u32[]{:S(2)}) copy-start(s32[1,1,16,2,2048]{4,3,2,1,0:T(2,128)} %param.10) | copy-start | bytes 786436
  39.6 1.6 %copy-start.3 = (f32[1,1,1,16,2,2048]{5,4,3,2,1,0:T(2,128)}, f32[1,1,1,16,2,2048]{5,4,3,2,1,0:T(2,128)S(1)}, u32[]{:S(2)}) copy-start(f32[1,1,1,16,2,2048]{5,4,3,2,1,0:T(2,128)S(1)} %get-tuple-element.61) | copy-start | bytes 786436
  39.6 1.6 %copy-start.6 = (f32[1,1,1,16,2,2048]{5,4,3,2,1,0:T(2,128)}, f32[1,1,1,16,2,2048]{5,4,3,2,1,0:T(2,128)S(1)}, u32[]{:S(2)}) copy-start(f32[1,1,1,16,2,2048]{5,4,3,2,1,0:T(2,128)S(1)} %get-tuple-element.62) | copy-start | bytes 786436
  39.8 1.9 %copy-start.13 = (f32[16,2,2048]{2,0,1:T(8,128)}, f32[16,2,2048]{2,0,1:T(8,128)S(1)}, u32[]{:S(2)}) copy-start(f32[16,2,2048]{2,0,1:T(8,128)S(1)} %fusion.81) | copy-start | bytes 786436
  48.4 10.1 %copy-start.17 = (f32[8,16,2048]{2,1,0:T(8,128)S(1)}, f32[8,16,2048]{2,1,0:T(8,128)}, u32[]{:S(2)}) copy-start(f32[8,16,2048]{2,1,0:T(8,128)} %get-tuple-element.23) | copy-start | bytes 3145732
  52.6 22.2 %copy-start.23 = (f32[8,8]{1,0:T(8,128)}, f32[8,8]{1,0:T(8,128)S(1)}, u32[]{:S(2)}) copy-start(f32[8,8]{1,0:T(8,128)S(1)} %fusion.120) | copy-start | bytes 772
  53.5 11.0 %all-to-all-start.1 = ((f32[8,1,2048]{2,1,0:T(1,128)}), f32[8,1,2048]{2,1,0:T(1,128)S(1)}, u32[]{:S(2)}, u32[]{:S(2)}) async-start(f32[8,1,2048]{2,1,0:T(1,128)} %copy.78), calls=%async_computation.1 | async-start | bytes 131072 | tf_op jit(solution)/shard_map/all_to_all | solution.py:119
  75.6 9.2 %all-to-all-start.3 = ((f32[8,1,2048]{2,1,0:T(1,128)}), f32[8,1,2048]{2,1,0:T(1,128)S(1)}, u32[]{:S(2)}, u32[]{:S(2)}) async-start(f32[8,1,2048]{2,1,0:T(1,128)} %copy.80), calls=%async_computation.3 | async-start | bytes 131072 | tf_op jit(solution)/shard_map/all_to_all | solution.py:119
  79.0 18.0 %copy-start.25 = (s32[4,40]{1,0:T(4,128)}, s32[4,40]{1,0:T(4,128)S(1)}, u32[]{:S(2)}) copy-start(s32[4,40]{1,0:T(4,128)S(1)} %dynamic-slice_bitcast_fusion) | copy-start | bytes 1924
  86.2 9.4 %all-to-all-start.4 = ((f32[4,40,512]{2,1,0:T(8,128)}), f32[4,40,512]{2,1,0:T(8,128)S(1)}, u32[]{:S(2)}, u32[]{:S(2)}) async-start(f32[4,40,512]{2,1,0:T(8,128)} %fusion.79), calls=%async_computation.4 | async-start | bytes 655360 | tf_op jit(solution)/shard_map/all_to_all | solution.py:146
  90.1 8.0 %copy-start.27 = (f32[64]{0:T(128)}, f32[64]{0:T(128)S(1)}, u32[]{:S(2)}) copy-start(f32[64]{0:T(128)S(1)} %broadcast_add_fusion) | copy-start | bytes 772
  105.7 2.9 %copy-start.4 = (f32[1,1,1,16,2,2048]{5,4,3,2,1,0:T(2,128)S(1)}, f32[1,1,1,16,2,2048]{5,4,3,2,1,0:T(2,128)}, u32[]{:S(2)}) copy-start(f32[1,1,1,16,2,2048]{5,4,3,2,1,0:T(2,128)} %copy-done.3) | copy-start | bytes 786436
  105.7 2.9 %copy-start.7 = (f32[1,1,1,16,2,2048]{5,4,3,2,1,0:T(2,128)S(1)}, f32[1,1,1,16,2,2048]{5,4,3,2,1,0:T(2,128)}, u32[]{:S(2)}) copy-start(f32[1,1,1,16,2,2048]{5,4,3,2,1,0:T(2,128)} %copy-done.6) | copy-start | bytes 786436
  105.7 3.4 %copy-start.18 = (f32[256,64]{1,0:T(8,128)S(1)}, f32[256,64]{1,0:T(8,128)}, u32[]{:S(2)}) copy-start(f32[256,64]{1,0:T(8,128)} %copy.84) | copy-start | bytes 196612
  105.7 3.4 %copy-start.10 = (f32[128,2048]{1,0:T(8,128)S(1)}, f32[128,2048]{1,0:T(8,128)}, u32[]{:S(2)}) copy-start(f32[128,2048]{1,0:T(8,128)} %get-tuple-element.54) | copy-start | bytes 3145732
  105.7 3.4 %copy-start.11 = (f32[128,2048]{1,0:T(8,128)S(1)}, f32[128,2048]{1,0:T(8,128)}, u32[]{:S(2)}) copy-start(f32[128,2048]{1,0:T(8,128)} %get-tuple-element.51) | copy-start | bytes 3145732
  105.7 3.4 %copy-start.12 = (f32[128,2048]{1,0:T(8,128)S(1)}, f32[128,2048]{1,0:T(8,128)}, u32[]{:S(2)}) copy-start(f32[128,2048]{1,0:T(8,128)} %get-tuple-element.52) | copy-start | bytes 3145732
  105.7 3.4 %copy-start.14 = (f32[16,2,2048]{2,0,1:T(8,128)S(1)}, f32[16,2,2048]{2,0,1:T(8,128)}, u32[]{:S(2)}) copy-start(f32[16,2,2048]{2,0,1:T(8,128)} %copy-done.13) | copy-start | bytes 786436
  108.5 1.5 copy-start.9
  115.0 1.6 %copy-start.22 = (s32[1,1,2048]{2,1,0:T(1,128)S(1)}, s32[1,1,2048]{2,1,0:T(1,128)}, u32[]{:S(2)}) copy-start(s32[1,1,2048]{2,1,0:T(1,128)} %copy-done.21) | copy-start | bytes 24580
  116.6 1.8 %copy-start.20 = (f32[256,64]{0,1:T(8,128)S(1)}, f32[256,64]{0,1:T(8,128)}, u32[]{:S(2)}) copy-start(f32[256,64]{0,1:T(8,128)} %get-tuple-element.75) | copy-start | bytes 196612
  116.6 10.4 %copy-start.24 = (f32[8,8]{1,0:T(8,128)S(1)}, f32[8,8]{1,0:T(8,128)}, u32[]{:S(2)}) copy-start(f32[8,8]{1,0:T(8,128)} %copy-done.23) | copy-start | bytes 772
  118.2 19.2 %copy-start.26 = (s32[4,40]{1,0:T(4,128)S(1)}, s32[4,40]{1,0:T(4,128)}, u32[]{:S(2)}) copy-start(s32[4,40]{1,0:T(4,128)} %copy-done.25) | copy-start | bytes 1924
  118.3 28.6 %copy-start.28 = (f32[64]{0:T(128)S(1)}, f32[64]{0:T(128)}, u32[]{:S(2)}) copy-start(f32[64]{0:T(128)} %copy-done.27) | copy-start | bytes 772
  127.9 9.2 %all-to-all-start.6 = ((f32[8,1,2048]{2,1,0:T(1,128)}), f32[8,1,2048]{2,1,0:T(1,128)S(1)}, u32[]{:S(2)}, u32[]{:S(2)}) async-start(f32[8,1,2048]{2,1,0:T(1,128)} %copy.87), calls=%async_computation.6 | async-start | bytes 131072 | tf_op jit(solution)/shard_map/all_to_all | solution.py:119
  149.8 1.5 copy-start.5
  (2 other events, 2.7 us)
where the time goes:
time: 156 us; the launch traced here: 155 us
  blocking collectives  26.1 us (17%)
  other arithmetic  24.3 us (16%)
  between operations  23.8 us (15%)
  starting transfers between devices  22.1 us (14%)
  matrix products  20.3 us (13%)
  local copies, waits for them, and re-layouts  19 us (12%)
  waiting for transfers between devices  18.9 us (12%)
    all_to_all x2, blocking collectives, consensus_values(): lax.all_to_all(rows, 'chan', split_axis=1, concat_axis=0, tiled=True)  17 us
    all_to_all x3, waiting for transfers between devices, consensus_values(): lax.all_to_all(smooth, 'chan', split_axis=0, concat_axis=1, tiled=True)  13.3 us
    all_to_all x3, starting transfers between devices, consensus_values(): lax.all_to_all(smooth, 'chan', split_axis=0, concat_axis=1, tiled=True)  12 us
    reduce_sum x2, other arithmetic, station_sides(): jnp.sum(resid_re * ups_re + resid_im * ups_im, axis=-2)  11.6 us
    dot_general x4, matrix products, to_stations(): jnp.dot(flat, receiver_choice_matrix, precision=high)  9.33 us
    all_to_all x1, blocking collectives, on_device(): lax.all_to_all(outgoing, 'grp', split_axis=0, concat_axis=0, tiled=True)  9.05 us
    dot_general x6, matrix products, spread_over_interferometer_pairs(): lax.dot_general(flat, receiver_choice_matrix, (((1,), (1,)), ((), ())), p...  7 us
    all_to_all x1, starting transfers between devices, consensus_values(): lax.all_to_all(rows, 'chan', split_axis=1, concat_axis=0, tiled=True)  6.35 us
  transfers between devices with their start and end apart: 5, of which 4 were waited for; matrix products, arithmetic and copies ran while one was open for 16% of the time, Pallas kernels for 0%

commit v1 on v0

v1 whole, which is shorter than its diff:
```python
import functools

import jax
import jax.numpy as jnp
import numpy as np
from jax import lax
from jax.experimental import pallas as pl
from jax.experimental.pallas import tpu as pltpu
from jax.sharding import PartitionSpec as P

ITERS = 2
FITS = ITERS + 1
F32 = jnp.float32
BF16 = jnp.bfloat16


def gram_inverse(count):
    xval = (2.0 * np.arange(count) + 1.0) / count - 1.0
    basis = np.stack([np.ones_like(xval), xval, 1.5 * xval * xval - 0.5], axis=1)
    gram = basis.T @ basis
    cross = [np.cross(gram[1], gram[2]), np.cross(gram[2], gram[0]), np.cross(gram[0], gram[1])]
    return np.stack(cross, axis=1) / np.sum(gram[0] * cross[0])


def halves(values):
    high = values.astype(BF16)
    return high, (values - high.astype(F32)).astype(BF16)


def nt_dot(left, right):
    return lax.dot_general(left, right, (((1,), (1,)), ((), ())), preferred_element_type=F32)


def kernel(
    groups, chans, dirs, block, rho,
    mod, vis, flg, ant, corr, gin,
    jout, zout, rout,
    pick, both, tmat, ghl, gath, prods, dsum, whl, acc, jcur, dual, zcur,
    xsend, xall, ssend, zbuf, jsend, jrecv,
    fit_send, fit_recv, grp_send, grp_recv,
):
    grp = lax.axis_index("grp")
    me = lax.axis_index("chan")
    samples, si, lines = flg.shape
    slots = gin.shape[-1]
    steps = lines // block
    rows = xsend.shape[2]
    ginv = gram_inverse(chans)

    def chan_peer(d):
        return lax.rem(me + d, chans)

    def grp_peer(d):
        return lax.rem(grp + d, groups)

    barrier = pltpu.get_barrier_semaphore()

    def greet(d, carry):
        pl.semaphore_signal(barrier, inc=1, device_id={"chan": chan_peer(d)}, device_id_type=pl.DeviceIdType.MESH)
        return carry

    lax.fori_loop(1, chans, greet, 0)
    for d in range(1, groups):
        pl.semaphore_signal(barrier, inc=1, device_id={"grp": grp_peer(d)}, device_id_type=pl.DeviceIdType.MESH)

    jcur[:, :slots] = gin[0]
    jcur[:, slots:] = gin[1]
    dual[...] = jnp.zeros_like(dual)

    pl.semaphore_wait(barrier, chans - 1 + groups - 1)

    def spread(fit, phase, source, target):
        def send(d, carry):
            peer = chan_peer(d)
            pltpu.make_async_remote_copy(
                src_ref=source.at[fit, peer],
                dst_ref=target.at[fit, me],
                send_sem=fit_send.at[fit, phase],
                recv_sem=fit_recv.at[fit, phase],
                device_id={"chan": peer},
                device_id_type=pl.DeviceIdType.MESH,
            ).start()
            return carry

        lax.fori_loop(1, chans, send, 0)
        target[fit, me] = source[fit, me]

    def landed(fit, phase, source, target):
        pltpu.make_async_copy(source.at[fit, pl.ds(0, chans - 1)], source.at[fit, pl.ds(0, chans - 1)], fit_send.at[fit, phase]).wait()
        pltpu.make_async_copy(target.at[fit, pl.ds(0, chans - 1)], target.at[fit, pl.ds(0, chans - 1)], fit_recv.at[fit, phase]).wait()

    def fit_begin(fit):
        def fill(f, carry):
            part = pl.ds(pl.multiple_of(f * rows, rows), rows)
            xsend[fit, f] = jcur[part, :] + dual[part, :]
            return carry

        lax.fori_loop(0, chans, fill, 0)
        spread(fit, 0, xsend, xall)

    def basis_of(f):
        xval = (2 * f + 1).astype(F32) * (1.0 / chans) - 1.0
        return xval, 1.5 * xval * xval - 0.5

    def fit_middle(fit):
        landed(fit, 0, xsend, xall)

        def gather(f, sums):
            first, second = basis_of(f)
            value = xall[fit, f]
            return sums[0] + value, sums[1] + first * value, sums[2] + second * value

        zero = jnp.zeros(xall.shape[2:], F32)
        sums = lax.fori_loop(0, chans, gather, (zero, zero, zero))
        coef = [sum(float(ginv[n, m]) * sums[m] for m in range(3)) for n in range(3)]

        def expand(f, carry):
            first, second = basis_of(f)
            ssend[fit, f] = coef[0] + first * coef[1] + second * coef[2]
            return carry

        lax.fori_loop(0, chans, expand, 0)
        spread(fit, 1, ssend, zbuf)

    def fit_end(fit):
        landed(fit, 1, ssend, zbuf)

        def place(f, carry):
            zcur[pl.ds(pl.multiple_of(f * rows, rows), rows), :] = zbuf[fit, f]
            return carry

        lax.fori_loop(0, chans, place, 0)

    fit_begin(0)

    def build(step, carry):
        cols = pl.ds(pl.multiple_of(step * block, block), block)
        station = lax.broadcasted_iota(jnp.int32, (slots, block), 0)
        for side in range(2):
            hot = (station == ant[pl.ds(side, 1), cols]).astype(F32).astype(BF16)
            zero = jnp.zeros_like(hot)
            for part in range(2):
                for half in range(2):
                    base = 2 * slots * half
                    pick[side, part, base + part * slots : base + (part + 1) * slots, cols] = hot
                    base += (1 - part) * slots
                    pick[side, part, base : base + slots, cols] = zero
                both[side, part * slots : (part + 1) * slots, cols] = hot
        return carry

    lax.fori_loop(0, steps, build, 0)

    listed = corr.shape[-1]
    row = lax.broadcasted_iota(jnp.int32, (2 * slots, listed), 0)
    row = jnp.where(row >= slots, row - slots, row)
    block_row = lax.broadcasted_iota(jnp.int32, (2 * slots, 2 * slots), 0) >= slots
    block_col = lax.broadcasted_iota(jnp.int32, (2 * slots, 2 * slots), 1) >= slots
    count = jnp.zeros((1, 2 * slots), F32)
    for d in range(1, groups):
        other = grp_peer(d)
        mine = (row == corr[grp, pl.ds(other, 1), :]).astype(F32).astype(BF16)
        theirs = (row == corr[other, pl.ds(grp, 1), :]).astype(F32).astype(BF16)
        table = jnp.where(block_row == block_col, nt_dot(theirs, mine), 0.0).astype(BF16)
        tmat[d - 1, : 2 * slots, :] = table
        tmat[d - 1, 2 * slots :, :] = table
        count = count + nt_dot(jnp.ones((8, listed), BF16), mine)[:1]

    def split_gains():
        high, low = halves(jcur[...])
        ghl[:, : 2 * slots] = high
        ghl[:, 2 * slots :] = low

    def residual_of(cols):
        for side in range(2):
            for part in range(2):
                gath[side, part] = jnp.dot(ghl[...], pick[side, part, :, cols], preferred_element_type=F32)
        total = [[jnp.zeros((si, block), F32) for _ in range(2)] for _ in range(samples)]
        for k in range(dirs):
            at = slice(k * si, (k + 1) * si)
            are, aim, cre, cim = gath[0, 0, at], gath[0, 1, at], gath[1, 0, at], gath[1, 1, at]
            pre = are * cre + aim * cim
            pim = aim * cre - are * cim
            for t in range(samples):
                mre = mod[0, t, at, cols].astype(F32)
                mim = mod[1, t, at, cols].astype(F32)
                total[t][0] += pre * mre - pim * mim
                total[t][1] += pre * mim + pim * mre
        res, weights = [], []
        for t in range(samples):
            weight = (1 - flg[t, :, cols]).astype(F32)
            weights.append(weight)
            res.append([weight * (vis[part, t, :, cols] - total[t][part]) for part in range(2)])
        return res, weights

    def update_block(first, step, carry):
        cols = pl.ds(pl.multiple_of(step * block, block), block)
        res, weights = residual_of(cols)
        for k in range(dirs):
            at = slice(k * si, (k + 1) * si)
            low_at = slice((dirs + k) * si, (dirs + k + 1) * si)
            rre = rim = dd = 0.0
            for t in range(samples):
                mre = mod[0, t, at, cols].astype(F32)
                mim = mod[1, t, at, cols].astype(F32)
                rre += res[t][0] * mre + res[t][1] * mim
                rim += res[t][1] * mre - res[t][0] * mim
                if first:
                    dd += weights[t] * (mre * mre + mim * mim)
            if first:
                dsum[at, cols] = dd
            else:
                dd = dsum[at, cols]
            are, aim, cre, cim = gath[0, 0, at], gath[0, 1, at], gath[1, 0, at], gath[1, 1, at]
            sums = (
                rre * cre - rim * cim,
                rre * cim + rim * cre,
                dd * (cre * cre + cim * cim),
                rre * are + rim * aim,
                rre * aim - rim * are,
                dd * (are * are + aim * aim),
            )
            for i, value in enumerate(sums):
                high, low = halves(value)
                whl[i, at] = high
                whl[i, low_at] = low
        grad = den = None
        for side in range(2):
            for part in range(2):
                piece = nt_dot(whl[3 * side + part], pick[side, part, : 2 * slots, cols])
                grad = piece if grad is None else grad + piece
            piece = nt_dot(whl[3 * side + 2], both[side, :, cols])
            den = piece if den is None else den + piece
        acc[0] += grad
        acc[1] += den
        return carry

    def residual_block(step, carry):
        cols = pl.ds(pl.multiple_of(step * block, block), block)
        res, _ = residual_of(cols)
        for t in range(samples):
            for part in range(2):
                rout[part, t, :, cols] = res[t][part]
        return carry

    count_rows = dirs * si
    for it in range(ITERS):
        split_gains()
        acc[...] = jnp.zeros_like(acc)
        body = functools.partial(update_block, it == 0)
        middle = steps // 2
        lax.fori_loop(0, middle, body, 0)
        fit_middle(it)
        lax.fori_loop(middle, steps, body, 0)
        fit_end(it)
        present = jcur[...]
        if it > 0:
            dual[...] = dual[...] + present - zcur[...]
        den = acc[1, :count_rows] + acc[1, count_rows:]
        num = acc[0, :count_rows] + acc[0, count_rows:] + present * den
        updated = (num + rho * (zcur[...] - dual[...])) / (den + rho)
        jsend[it] = updated
        copies = []
        for d in range(1, groups):
            copy = pltpu.make_async_remote_copy(
                src_ref=jsend.at[it],
                dst_ref=jrecv.at[it, groups - d - 1],
                send_sem=grp_send.at[it, d - 1],
                recv_sem=grp_recv.at[it, groups - d - 1],
                device_id={"grp": grp_peer(d)},
                device_id_type=pl.DeviceIdType.MESH,
            )
            copy.start()
            copies.append(copy)
        total = updated
        for d in range(1, groups):
            pltpu.make_async_copy(jrecv.at[it, d - 1], jrecv.at[it, d - 1], grp_recv.at[it, d - 1]).wait()
            high, low = halves(jrecv[it, d - 1])
            total = total + jnp.dot(jnp.concatenate([high, low], axis=1), tmat[d - 1], preferred_element_type=F32)
        for copy in copies:
            copy.wait_send()
        jcur[...] = total / (1.0 + count)
        fit_begin(it + 1)

    split_gains()
    jout[0] = jcur[:, :slots]
    jout[1] = jcur[:, slots:]
    middle = steps // 2
    lax.fori_loop(0, middle, residual_block, 0)
    fit_middle(ITERS)
    lax.fori_loop(middle, steps, residual_block, 0)
    fit_end(ITERS)
    zout[0] = zcur[:, :slots]
    zout[1] = zcur[:, slots:]


def on_device(groups, chans, visibilities, model, flags, antennas, correlation, gains_init):
    _, _, dirs, _, si, samples, lines = model.shape
    slots = gains_init.shape[-1]
    count = dirs * si
    rho = 2.0 * lines * samples / slots
    block = min(256, lines)
    rows = count // chans
    mod = jnp.transpose(model[0, :, :, 0], (0, 3, 1, 2, 4)).reshape(2, samples, count, lines)
    vis = jnp.transpose(visibilities[0, :, 0], (0, 2, 1, 3))
    flg = jnp.transpose(flags[0, 0], (1, 0, 2))
    gin = gains_init.reshape(2, count, slots)
    vmem = pl.BlockSpec(memory_space=pltpu.VMEM)
    wide = 2 * slots
    jones, agreed, res = pl.pallas_call(
        functools.partial(kernel, groups, chans, dirs, block, rho),
        out_shape=(
            jax.ShapeDtypeStruct((2, count, slots), F32),
            jax.ShapeDtypeStruct((2, count, slots), F32),
            jax.ShapeDtypeStruct((2, samples, si, lines), F32),
        ),
        in_specs=[vmem] * 6,
        out_specs=(vmem, vmem, vmem),
        scratch_shapes=[
            pltpu.VMEM((2, 2, 2 * wide, lines), BF16),
            pltpu.VMEM((2, wide, lines), BF16),
            pltpu.VMEM((groups - 1, 2 * wide, wide), BF16),
            pltpu.VMEM((count, 2 * wide), BF16),
            pltpu.VMEM((2, 2, count, block), F32),
            pltpu.VMEM((2, count, block), F32),
            pltpu.VMEM((count, lines), F32),
            pltpu.VMEM((6, 2 * count, block), BF16),
            pltpu.VMEM((2, 2 * count, wide), F32),
            pltpu.VMEM((count, wide), F32),
            pltpu.VMEM((count, wide), F32),
            pltpu.VMEM((count, wide), F32),
            pltpu.VMEM((FITS, chans, rows, wide), F32),
            pltpu.VMEM((FITS, chans, rows, wide), F32),
            pltpu.VMEM((FITS, chans, rows, wide), F32),
            pltpu.VMEM((FITS, chans, rows, wide), F32),
            pltpu.VMEM((ITERS, count, wide), F32),
            pltpu.VMEM((ITERS, groups - 1, count, wide), F32),
            pltpu.SemaphoreType.DMA((FITS, 2)),
            pltpu.SemaphoreType.DMA((FITS, 2)),
            pltpu.SemaphoreType.DMA((ITERS, groups - 1)),
            pltpu.SemaphoreType.DMA((ITERS, groups - 1)),
        ],
        compiler_params=pltpu.CompilerParams(
            collective_id=0, has_side_effects=True, vmem_limit_bytes=48 * 1024 * 1024
        ),
    )(mod, vis, flg, antennas[0], correlation, gin)
    res = jnp.transpose(res, (0, 2, 1, 3))
    return (
        jones.reshape(gains_init.shape),
        agreed.reshape(gains_init.shape),
        res.reshape(visibilities.shape),
    )


def solution(mesh):
    return jax.shard_map(
        functools.partial(on_device, mesh.shape["grp"], mesh.shape["chan"]),
        mesh=mesh,
        in_specs=(
            P("grp", None, "chan", None, None, None),
            P("grp", None, None, "chan", None, None, None),
            P("grp", "chan", None, None, None),
            P("grp", None, None),
            P(),
            P("grp", None, None, "chan", None, None),
        ),
        out_specs=(
            P("grp", None, None, "chan", None, None),
            P("grp", None, None, "chan", None, None),
            P("grp", None, "chan", None, None, None),
        ),
        check_vma=False,
    )
```

time: 156 us -> 48.5 us (0.31)
  Pallas kernels: 0 us -> 40.1 us
  blocking collectives: 26.1 us -> 0 us
  other arithmetic: 24.3 us -> 0 us
  between operations: 23.8 us -> 0.69 us
  starting transfers between devices: 22.1 us -> 0 us
  matrix products: 20.3 us -> 0 us
  waiting for transfers between devices: 18.9 us -> 0 us
  local copies, waits for them, and re-layouts: 19 us -> 7.52 us
    pallas_call x0 -> x1, Pallas kernels: none -> 40.1 us  [on_device(): pl.pallas_call(functools.partial(kernel, groups, chans, dirs, block, rho)...]
    all_to_all x3 -> x0, blocking collectives: 26.1 us -> none  [the longest x2 17 us: consensus_values(): lax.all_to_all(rows, 'chan', split_axis=1, concat_axis=0, tiled=True)]
    all_to_all x5 -> x0, starting transfers between devices: 22.1 us -> none  [the longest x3 12 us: consensus_values(): lax.all_to_all(smooth, 'chan', split_axis=0, concat_axis=1, tiled=True)]
    dot_general x20 -> x0, matrix products: 20.3 us -> none  [the longest x4 9.33 us: to_stations(): jnp.dot(flat, receiver_choice_matrix, precision=high)]
    all_to_all x5 -> x0, waiting for transfers between devices: 18.9 us -> none  [the longest x3 13.3 us: consensus_values(): lax.all_to_all(smooth, 'chan', split_axis=0, concat_axis=1, tiled=True)]
    reduce_sum x7 -> x0, other arithmetic: 18 us -> none  [the longest x2 11.6 us: station_sides(): jnp.sum(resid_re * ups_re + resid_im * ups_im, axis=-2)]
    slice x15 -> x0, local copies, waits for them, and re-layouts: 11.7 us -> none  [the longest x2 2.35 us: on_device(): present_jones_matrices = joined[:gain_rows.shape[0]].reshape(updated.shape)]
    all_to_all x5 -> x0, local copies, waits for them, and re-layouts: 3.94 us -> none  [the longest x3 2.09 us: consensus_values(): lax.all_to_all(smooth, 'chan', split_axis=0, concat_axis=1, tiled=True)]
  transfers between devices with their start and end apart: 5 -> 0, of which waited for: 4 -> 0; matrix products, arithmetic and copies ran while one was open for 16% -> 0% of each run, Pallas kernels for 0% -> 0%
where the time goes in v1:
time: 48.5 us; the launch traced here: 48.3 us
  Pallas kernels  40.1 us (83%)
  local copies, waits for them, and re-layouts  7.52 us (16%)
  between operations  0.69 us (1%)
    pallas_call x1, Pallas kernels, on_device(): pl.pallas_call(functools.partial(kernel, groups, chans, dirs, block, rho)...  40.1 us
    unnamed x11, local copies, waits for them, and re-layouts  4.99 us
    transpose x1, local copies, waits for them, and re-layouts, on_device(): jnp.transpose(model[0, :, :, 0], (0, 3, 1, 2, 4))  2.53 us

profile of v1, /device:TPU:0, one launch (start us, length us, event | category | flops | bytes accessed | tf_op | source)
XLA Modules:
  0.0 48.3 jit_solution(16700607082616498653)
XLA Ops:
  0.6 1.1 %copy.18 = s32[1,1,16,2,2048]{4,2,3,1,0:T(8,128)S(1)} copy(s32[1,1,16,2,2048]{4,3,2,1,0:T(2,128)} %param.8) | data formatting | bytes 524288 | tf_op args[2]
  1.7 1.4 %copy.17 = f32[1,2,1,16,2,2048]{5,3,4,1,2,0:T(8,128)S(1)} copy(f32[1,2,1,16,2,2048]{5,4,3,2,1,0:T(2,128)} %param.6) | data formatting | bytes 1048576 | tf_op args[0]
  3.1 0.0 copy-start
  3.1 0.0 copy-start.1
  3.1 0.0 copy-start.2
  3.1 2.5 %copy.9 = bf16[2,2,8,16,2048]{4,3,2,1,0:T(8,128)(2,1)S(1)} copy(bf16[2,2,8,16,2048]{4,1,3,2,0:T(2,128)(2,1)} %bitcast.33) | data formatting | bytes 4194304 | tf_op jit(solution)/shard_map/transpose | solution.py:303
  5.7 0.0 copy-done
  5.7 0.0 copy-done.1
  5.7 0.0 copy-done.2
  5.7 40.1 %shard_map.85 = (f32[2,128,64]{2,1,0:T(8,128)S(1)}, f32[2,128,64]{2,1,0:T(8,128)S(1)}, f32[2,2,16,2048]{3,2,1,0:T(8,128)S(1)}) custom-call(bf16[2,2,128,2048]{3,2,1,0:T(8,128)(2,1)S(1)} %bitcast.25, f32[2,2,16,2048]{3,2,1,0:T(8,128)S(1)} %bitcast.26, s32[2,16,2048]{2,1,0:T(8,128)S(1)} %bitcast.27, s32[2,2048]{1,0:T(2,128)S(1)} %bitcast.32, ...), custom_call_target="tpu_custom_call" | custom-call | tf_op jit(solution)/shard_map/pallas_call | solution.py:309
  45.8 1.2 %copy.14 = f32[1,2,1,16,2,2048]{5,4,3,2,1,0:T(2,128)} copy(f32[1,2,1,16,2,2048]{5,3,4,1,2,0:T(8,128)S(1)} %bitcast.28) | data formatting | bytes 1048576
  47.0 0.7 %copy.21 = f32[1,2,8,1,16,64]{5,4,3,2,1,0:T(8,128)} copy(f32[1,2,8,1,16,64]{5,4,3,2,1,0:T(8,128)S(1)} %bitcast.31) | data formatting | bytes 131072
  47.6 0.7 %copy.22 = f32[1,2,8,1,16,64]{5,4,3,2,1,0:T(8,128)} copy(f32[1,2,8,1,16,64]{5,4,3,2,1,0:T(8,128)S(1)} %bitcast.30) | data formatting | bytes 131072
Async XLA Ops:
  3.1 2.6 %copy-start = (f32[1,2,8,1,16,64]{5,4,3,2,1,0:T(8,128)S(1)}, f32[1,2,8,1,16,64]{5,4,3,2,1,0:T(8,128)}, u32[]{:S(2)}) copy-start(f32[1,2,8,1,16,64]{5,4,3,2,1,0:T(8,128)} %param.11) | copy-start | bytes 196612
  3.1 2.6 %copy-start.1 = (s32[1,2,2048]{2,1,0:T(2,128)S(1)}, s32[1,2,2048]{2,1,0:T(2,128)}, u32[]{:S(2)}) copy-start(s32[1,2,2048]{2,1,0:T(2,128)} %param.9) | copy-start | bytes 49156
  3.1 2.6 %copy-start.2 = (s32[4,4,40]{2,1,0:T(4,128)S(1)}, s32[4,4,40]{2,1,0:T(4,128)}, u32[]{:S(2)}) copy-start(s32[4,4,40]{2,1,0:T(4,128)} %corr.1) | copy-start | bytes 7684

commit v2 on v1

--- a/solution.py
+++ b/solution.py
@@ -12,6 +12,7 @@
 FITS = ITERS + 1
 F32 = jnp.float32
 BF16 = jnp.bfloat16
+LANES = 128
 
 
 def gram_inverse(count):
@@ -41,7 +42,10 @@
 ):
     grp = lax.axis_index("grp")
     me = lax.axis_index("chan")
-    samples, si, lines = flg.shape
+    samples, count_rows, lines = mod.shape[1:]
+    si = count_rows // dirs
+    per = block // LANES
+    stride = lines // LANES * samples
     slots = gin.shape[-1]
     steps = lines // block
     rows = xsend.shape[2]
@@ -69,25 +73,35 @@
 
     pl.semaphore_wait(barrier, chans - 1 + groups - 1)
 
-    def spread(fit, phase, source, target):
-        def send(d, carry):
-            peer = chan_peer(d)
+    owners = xsend.shape[1]
+    least = (chans - owners) // 2
+    owner = (me >= least) & (me < least + owners)
+    mine_at = jnp.clip(me - least, 0, owners - 1)
+
+    def send_to(source, target, fit, phase, peer):
+        @pl.when(peer != me)
+        def _():
             pltpu.make_async_remote_copy(
-                src_ref=source.at[fit, peer],
-                dst_ref=target.at[fit, me],
+                src_ref=source,
+                dst_ref=target,
                 send_sem=fit_send.at[fit, phase],
                 recv_sem=fit_recv.at[fit, phase],
                 device_id={"chan": peer},
                 device_id_type=pl.DeviceIdType.MESH,
             ).start()
-            return carry
-
-        lax.fori_loop(1, chans, send, 0)
-        target[fit, me] = source[fit, me]
-
-    def landed(fit, phase, source, target):
-        pltpu.make_async_copy(source.at[fit, pl.ds(0, chans - 1)], source.at[fit, pl.ds(0, chans - 1)], fit_send.at[fit, phase]).wait()
-        pltpu.make_async_copy(target.at[fit, pl.ds(0, chans - 1)], target.at[fit, pl.ds(0, chans - 1)], fit_recv.at[fit, phase]).wait()
+
+    def took(ref, number, sem):
+        part = ref.at[pl.ds(0, number)]
+        pltpu.make_async_copy(part, part, sem).wait()
+
+    def took_by_role(ref, sem):
+        @pl.when(owner)
+        def _():
+            took(ref, owners - 1, sem)
+
+        @pl.when(jnp.logical_not(owner))
+        def _():
+            took(ref, owners, sem)
 
     def fit_begin(fit):
         def fill(f, carry):
@@ -95,41 +109,64 @@
             xsend[fit, f] = jcur[part, :] + dual[part, :]
             return carry
 
-        lax.fori_loop(0, chans, fill, 0)
-        spread(fit, 0, xsend, xall)
+        lax.fori_loop(0, owners, fill, 0)
+
+        def send(n, carry):
+            send_to(xsend.at[fit, n], xall.at[fit, me], fit, 0, least + n)
+            return carry
+
+        lax.fori_loop(0, owners, send, 0)
+
+        @pl.when(owner)
+        def _():
+            xall[fit, me] = xsend[fit, mine_at]
 
     def basis_of(f):
         xval = (2 * f + 1).astype(F32) * (1.0 / chans) - 1.0
         return xval, 1.5 * xval * xval - 0.5
 
     def fit_middle(fit):
-        landed(fit, 0, xsend, xall)
-
-        def gather(f, sums):
-            first, second = basis_of(f)
-            value = xall[fit, f]
-            return sums[0] + value, sums[1] + first * value, sums[2] + second * value
-
-        zero = jnp.zeros(xall.shape[2:], F32)
-        sums = lax.fori_loop(0, chans, gather, (zero, zero, zero))
-        coef = [sum(float(ginv[n, m]) * sums[m] for m in range(3)) for n in range(3)]
-
-        def expand(f, carry):
-            first, second = basis_of(f)
-            ssend[fit, f] = coef[0] + first * coef[1] + second * coef[2]
-            return carry
-
-        lax.fori_loop(0, chans, expand, 0)
-        spread(fit, 1, ssend, zbuf)
+        took_by_role(xsend.at[fit], fit_send.at[fit, 0])
+
+        @pl.when(owner)
+        def _():
+            took(xall.at[fit], chans - 1, fit_recv.at[fit, 0])
+
+            def gather(f, sums):
+                first, second = basis_of(f)
+                value = xall[fit, f]
+                return sums[0] + value, sums[1] + first * value, sums[2] + second * value
+
+            zero = jnp.zeros(xall.shape[2:], F32)
+            sums = lax.fori_loop(0, chans, gather, (zero, zero, zero))
+            coef = [sum(float(ginv[n, m]) * sums[m] for m in range(3)) for n in range(3)]
+
+            def expand(f, carry):
+                first, second = basis_of(f)
+                ssend[fit, f] = coef[0] + first * coef[1] + second * coef[2]
+                return carry
+
+            lax.fori_loop(0, chans, expand, 0)
+
+            def send(f, carry):
+                send_to(ssend.at[fit, f], zbuf.at[fit, mine_at], fit, 1, f)
+                return carry
+
+            lax.fori_loop(0, chans, send, 0)
+            zbuf[fit, mine_at] = ssend[fit, me]
 
     def fit_end(fit):
-        landed(fit, 1, ssend, zbuf)
+        took_by_role(zbuf.at[fit], fit_recv.at[fit, 1])
+
+        @pl.when(owner)
+        def _():
+            took(ssend.at[fit], chans - 1, fit_send.at[fit, 1])
 
         def place(f, carry):
             zcur[pl.ds(pl.multiple_of(f * rows, rows), rows), :] = zbuf[fit, f]
             return carry
 
-        lax.fori_loop(0, chans, place, 0)
+        lax.fori_loop(0, owners, place, 0)
 
     fit_begin(0)
 
@@ -151,26 +188,33 @@
     lax.fori_loop(0, steps, build, 0)
 
     listed = corr.shape[-1]
-    row = lax.broadcasted_iota(jnp.int32, (2 * slots, listed), 0)
+    wide = 2 * slots
+    row = lax.broadcasted_iota(jnp.int32, (wide, 2 * listed), 0)
+    place = lax.broadcasted_iota(jnp.int32, (wide, 2 * listed), 1)
+    same = (row >= slots) == (place >= listed)
     row = jnp.where(row >= slots, row - slots, row)
-    block_row = lax.broadcasted_iota(jnp.int32, (2 * slots, 2 * slots), 0) >= slots
-    block_col = lax.broadcasted_iota(jnp.int32, (2 * slots, 2 * slots), 1) >= slots
-    count = jnp.zeros((1, 2 * slots), F32)
+    eye = lax.broadcasted_iota(jnp.int32, (2 * listed, 2 * listed), 0) == lax.broadcasted_iota(
+        jnp.int32, (2 * listed, 2 * listed), 1
+    )
+    eye = eye.astype(F32).astype(BF16)
     for d in range(1, groups):
-        other = grp_peer(d)
-        mine = (row == corr[grp, pl.ds(other, 1), :]).astype(F32).astype(BF16)
-        theirs = (row == corr[other, pl.ds(grp, 1), :]).astype(F32).astype(BF16)
-        table = jnp.where(block_row == block_col, nt_dot(theirs, mine), 0.0).astype(BF16)
-        tmat[d - 1, : 2 * slots, :] = table
-        tmat[d - 1, 2 * slots :, :] = table
-        count = count + nt_dot(jnp.ones((8, listed), BF16), mine)[:1]
+        mine = corr[grp, pl.ds(grp_peer(d), 1), :]
+        hot = (same & (row == jnp.concatenate([mine, mine], axis=1))).astype(F32).astype(BF16)
+        tmat[(d - 1) * 2 * listed : d * 2 * listed, :] = nt_dot(eye, hot).astype(BF16)
+    count = jnp.dot(jnp.ones((8, tmat.shape[0]), BF16), tmat[...], preferred_element_type=F32)[:1]
+
+    def lines_of(step, t):
+        return [pl.ds((step * per + p) * samples + t, si, stride=stride) for p in range(per)]
+
+    def read(ref, lead, step, t):
+        return jnp.concatenate([ref[(*lead, part, slice(None))] for part in lines_of(step, t)], axis=1)
 
     def split_gains():
         high, low = halves(jcur[...])
         ghl[:, : 2 * slots] = high
         ghl[:, 2 * slots :] = low
 
-    def residual_of(cols):
+    def residual_of(step, cols):
         for side in range(2):
             for part in range(2):
                 gath[side, part] = jnp.dot(ghl[...], pick[side, part, :, cols], preferred_element_type=F32)
@@ -187,14 +231,14 @@
                 total[t][1] += pre * mim + pim * mre
         res, weights = [], []
         for t in range(samples):
-            weight = (1 - flg[t, :, cols]).astype(F32)
+            weight = (1 - read(flg, (), step, t)).astype(F32)
             weights.append(weight)
-            res.append([weight * (vis[part, t, :, cols] - total[t][part]) for part in range(2)])
+            res.append([weight * (read(vis, (part,), step, t) - total[t][part]) for part in range(2)])
         return res, weights
 
     def update_block(first, step, carry):
         cols = pl.ds(pl.multiple_of(step * block, block), block)
-        res, weights = residual_of(cols)
+        res, weights = residual_of(step, cols)
         for k in range(dirs):
             at = slice(k * si, (k + 1) * si)
             low_at = slice((dirs + k) * si, (dirs + k + 1) * si)
@@ -236,13 +280,13 @@
 
     def residual_block(step, carry):
         cols = pl.ds(pl.multiple_of(step * block, block), block)
-        res, _ = residual_of(cols)
+        res, _ = residual_of(step, cols)
         for t in range(samples):
             for part in range(2):
-                rout[part, t, :, cols] = res[t][part]
+                for p, at in enumerate(lines_of(step, t)):
+                    rout[part, at, :] = res[t][part][:, p * LANES : (p + 1) * LANES]
         return carry
 
-    count_rows = dirs * si
     for it in range(ITERS):
         split_gains()
         acc[...] = jnp.zeros_like(acc)
@@ -258,11 +302,13 @@
         den = acc[1, :count_rows] + acc[1, count_rows:]
         num = acc[0, :count_rows] + acc[0, count_rows:] + present * den
         updated = (num + rho * (zcur[...] - dual[...])) / (den + rho)
-        jsend[it] = updated
+        high, low = halves(updated)
+        shared = nt_dot(tmat[...], high) + nt_dot(tmat[...], low)
         copies = []
         for d in range(1, groups):
+            jsend[it, d - 1] = shared[(d - 1) * 2 * listed : d * 2 * listed]
             copy = pltpu.make_async_remote_copy(
-                src_ref=jsend.at[it],
+                src_ref=jsend.at[it, d - 1],
                 dst_ref=jrecv.at[it, groups - d - 1],
                 send_sem=grp_send.at[it, d - 1],
                 recv_sem=grp_recv.at[it, groups - d - 1],
@@ -271,11 +317,12 @@
             )
             copy.start()
             copies.append(copy)
-        total = updated
         for d in range(1, groups):
             pltpu.make_async_copy(jrecv.at[it, d - 1], jrecv.at[it, d - 1], grp_recv.at[it, d - 1]).wait()
-            high, low = halves(jrecv[it, d - 1])
-            total = total + jnp.dot(jnp.concatenate([high, low], axis=1), tmat[d - 1], preferred_element_type=F32)
+        arrived = jnp.concatenate([jrecv[it, d] for d in range(groups - 1)], axis=0)
+        high, low = halves(arrived.T)
+        table = tmat[...]
+        total = updated + jnp.dot(high, table, preferred_element_type=F32) + jnp.dot(low, table, preferred_element_type=F32)
         for copy in copies:
             copy.wait_send()
         jcur[...] = total / (1.0 + count)
@@ -299,26 +346,34 @@
     count = dirs * si
     rho = 2.0 * lines * samples / slots
     block = min(256, lines)
-    rows = count // chans
+    owners = max(chans // 2, 1)
+    rows = count // owners
     mod = jnp.transpose(model[0, :, :, 0], (0, 3, 1, 2, 4)).reshape(2, samples, count, lines)
-    vis = jnp.transpose(visibilities[0, :, 0], (0, 2, 1, 3))
-    flg = jnp.transpose(flags[0, 0], (1, 0, 2))
+    tiles = lines // LANES
+
+    def natural(values, *lead):
+        split = values.reshape(*lead, si, samples, tiles, LANES)
+        return jnp.swapaxes(split, -2, -3).reshape(*lead, si * tiles * samples, LANES)
+
+    vis = natural(visibilities, 2)
+    flg = natural(flags)
     gin = gains_init.reshape(2, count, slots)
     vmem = pl.BlockSpec(memory_space=pltpu.VMEM)
     wide = 2 * slots
+    listed = correlation.shape[-1]
     jones, agreed, res = pl.pallas_call(
         functools.partial(kernel, groups, chans, dirs, block, rho),
         out_shape=(
             jax.ShapeDtypeStruct((2, count, slots), F32),
             jax.ShapeDtypeStruct((2, count, slots), F32),
-            jax.ShapeDtypeStruct((2, samples, si, lines), F32),
+            jax.ShapeDtypeStruct((2, si * tiles * samples, LANES), F32),
         ),
         in_specs=[vmem] * 6,
         out_specs=(vmem, vmem, vmem),
         scratch_shapes=[
             pltpu.VMEM((2, 2, 2 * wide, lines), BF16),
             pltpu.VMEM((2, wide, lines), BF16),
-            pltpu.VMEM((groups - 1, 2 * wide, wide), BF16),
+            pltpu.VMEM(((groups - 1) * 2 * listed, wide), BF16),
             pltpu.VMEM((count, 2 * wide), BF16),
             pltpu.VMEM((2, 2, count, block), F32),
             pltpu.VMEM((2, count, block), F32),
@@ -328,12 +383,12 @@
             pltpu.VMEM((count, wide), F32),
             pltpu.VMEM((count, wide), F32),
             pltpu.VMEM((count, wide), F32),
+            pltpu.VMEM((FITS, owners, rows, wide), F32),
             pltpu.VMEM((FITS, chans, rows, wide), F32),
             pltpu.VMEM((FITS, chans, rows, wide), F32),
-            pltpu.VMEM((FITS, chans, rows, wide), F32),
-            pltpu.VMEM((FITS, chans, rows, wide), F32),
-            pltpu.VMEM((ITERS, count, wide), F32),
-            pltpu.VMEM((ITERS, groups - 1, count, wide), F32),
+            pltpu.VMEM((FITS, owners, rows, wide), F32),
+            pltpu.VMEM((ITERS, groups - 1, 2 * listed, count), F32),
+            pltpu.VMEM((ITERS, groups - 1, 2 * listed, count), F32),
             pltpu.SemaphoreType.DMA((FITS, 2)),
             pltpu.SemaphoreType.DMA((FITS, 2)),
             pltpu.SemaphoreType.DMA((ITERS, groups - 1)),
@@ -343,7 +398,7 @@
             collective_id=0, has_side_effects=True, vmem_limit_bytes=48 * 1024 * 1024
         ),
     )(mod, vis, flg, antennas[0], correlation, gin)
-    res = jnp.transpose(res, (0, 2, 1, 3))
+    res = jnp.swapaxes(res.reshape(2, si, tiles, samples, LANES), -2, -3)
     return (
         jones.reshape(gains_init.shape),
         agreed.reshape(gains_init.shape),

time: 48.5 us -> 42.1 us (0.87)
  Pallas kernels: 40.1 us -> 36.6 us
  local copies, waits for them, and re-layouts: 7.52 us -> 4.67 us
    pallas_call x1, Pallas kernels: 40.1 us -> 36.6 us  [on_device(): pl.pallas_call(functools.partial(kernel, groups, chans, dirs, block, rho)...]
    unnamed x11 -> x13, local copies, waits for them, and re-layouts: 4.99 us -> 2.13 us
where the time goes in v2:
time: 42.1 us; the launch traced here: 42 us
  Pallas kernels  36.6 us (87%)
  local copies, waits for them, and re-layouts  4.67 us (11%)
  between operations  0.72 us (2%)
    pallas_call x1, Pallas kernels, on_device(): pl.pallas_call(functools.partial(kernel, groups, chans, dirs, block, rho)...  36.6 us
    transpose x1, local copies, waits for them, and re-layouts, on_device(): jnp.transpose(model[0, :, :, 0], (0, 3, 1, 2, 4))  2.54 us
    unnamed x13, local copies, waits for them, and re-layouts  2.13 us

profile of v2, /device:TPU:0, one launch (start us, length us, event | category | flops | bytes accessed | tf_op | source)
XLA Modules:
  0.0 42.0 jit_solution(8951459046557185704)
XLA Ops:
  0.6 0.0 copy-start
  0.6 0.0 copy-start.1
  0.7 0.0 copy-start.2
  0.7 0.0 copy-start.3
  0.7 0.0 copy-start.4
  0.7 2.5 %copy.9 = bf16[2,2,8,16,2048]{4,3,2,1,0:T(8,128)(2,1)S(1)} copy(bf16[2,2,8,16,2048]{4,1,3,2,0:T(2,128)(2,1)} %bitcast.35) | data formatting | bytes 4194304 | tf_op jit(solution)/shard_map/transpose | solution.py:351
  3.2 0.0 copy-done
  3.2 0.0 copy-done.1
  3.2 0.0 copy-done.2
  3.3 0.0 copy-done.3
  3.3 0.0 copy-done.4
  3.3 36.6 %shard_map.85 = (f32[2,128,64]{2,1,0:T(8,128)S(1)}, f32[2,128,64]{2,1,0:T(8,128)S(1)}, f32[2,512,128]{2,1,0:T(8,128)S(1)}) custom-call(bf16[2,2,128,2048]{3,2,1,0:T(8,128)(2,1)S(1)} %bitcast.27, f32[2,512,128]{2,1,0:T(8,128)S(1)} %bitcast.29, s32[512,128]{1,0:T(8,128)S(1)} %bitcast.30, s32[2,2048]{1,0:T(2,128)S(1)} %bitcast.34, s32[4,4,40]{2,1,0:T(4,128)S(1)} %copy-done.4, ...), custom_call_target="tpu_custom_call" | custom-call | tf_op jit(solution)/shard_map/pallas_call | solution.py:364
  39.9 0.7 %copy.18 = f32[1,2,8,1,16,64]{5,4,3,2,1,0:T(8,128)} copy(f32[1,2,8,1,16,64]{5,4,3,2,1,0:T(8,128)S(1)} %bitcast.33) | data formatting | bytes 131072
  40.5 0.7 %copy.19 = f32[1,2,8,1,16,64]{5,4,3,2,1,0:T(8,128)} copy(f32[1,2,8,1,16,64]{5,4,3,2,1,0:T(8,128)S(1)} %bitcast.32) | data formatting | bytes 131072
  41.2 0.8 %copy.20 = f32[1,2,1,16,2,2048]{5,4,3,2,1,0:T(2,128)} copy(f32[1,2,1,16,2,2048]{5,4,3,2,1,0:T(2,128)S(1)} %bitcast.28) | data formatting | bytes 1048576
Async XLA Ops:
  0.6 2.6 %copy-start = (f32[1,2,1,16,2,2048]{5,4,3,2,1,0:T(2,128)S(1)}, f32[1,2,1,16,2,2048]{5,4,3,2,1,0:T(2,128)}, u32[]{:S(2)}) copy-start(f32[1,2,1,16,2,2048]{5,4,3,2,1,0:T(2,128)} %param.6) | copy-start | bytes 1572868
  0.6 2.6 %copy-start.1 = (s32[1,1,16,2,2048]{4,3,2,1,0:T(2,128)S(1)}, s32[1,1,16,2,2048]{4,3,2,1,0:T(2,128)}, u32[]{:S(2)}) copy-start(s32[1,1,16,2,2048]{4,3,2,1,0:T(2,128)} %param.8) | copy-start | bytes 786436
  0.7 2.6 %copy-start.2 = (f32[1,2,8,1,16,64]{5,4,3,2,1,0:T(8,128)S(1)}, f32[1,2,8,1,16,64]{5,4,3,2,1,0:T(8,128)}, u32[]{:S(2)}) copy-start(f32[1,2,8,1,16,64]{5,4,3,2,1,0:T(8,128)} %param.11) | copy-start | bytes 196612
  0.7 2.6 %copy-start.3 = (s32[1,2,2048]{2,1,0:T(2,128)S(1)}, s32[1,2,2048]{2,1,0:T(2,128)}, u32[]{:S(2)}) copy-start(s32[1,2,2048]{2,1,0:T(2,128)} %param.9) | copy-start | bytes 49156
  0.7 2.6 %copy-start.4 = (s32[4,4,40]{2,1,0:T(4,128)S(1)}, s32[4,4,40]{2,1,0:T(4,128)}, u32[]{:S(2)}) copy-start(s32[4,4,40]{2,1,0:T(4,128)} %corr.1) | copy-start | bytes 7684
